TPU v7x, 32 devices: a whole 2x2x4 slice. The times are simulated.
32 devices in a mesh: dp: 4 (over x, core), section: 2 (over y), mp: 4 (over z).
Axes of the slice: x: 2, y: 2, z: 4, core: 2. Of those that a mesh axis runs over, the one named last changes fastest.
Arguments:
- micro_inputs: bfloat16 [8, 64, 4096], P(('dp', 'section'), None, 'mp'), parts along dimension 0, may hold values from -6 to 6
- qkv_weight: bfloat16 [2, 4096, 3, 2048], P('section', None, None, 'mp'), may hold values from -0.09375 to 0.09375
- out_weight: bfloat16 [2, 2048, 4096], P('section', None, 'mp'), may hold values from -0.125 to 0.125
- norm_gain: bfloat16 [2, 4096], P('section'), may hold values from 0.099609375 to 1.8984375
- position_bias: float32 [32, 32], P('mp'), may hold values from -3 to 280
Outputs:
- encoded: bfloat16 [8, 64, 4096], P(('dp', 'section'), None, 'mp'), parts along dimension 0
There are 4 independent parts, one for each index of `dp`. A program takes and returns all parts, laid end to end along the dimension named above; an argument that names none is the same for every part. Nothing has to cross between parts.
All inputs are finite; a program needn't handle non-finite values.
Results may differ from a plain program's by a relative error of at most 0.025.
Values may be sent and summed in bfloat16 or wider, within the bound.
A program may use at most 128 MiB of HBM per device.

v0:
```python
import functools
import math

import jax
import jax.numpy as jnp
import numpy as np
from jax import lax
from jax.experimental import pallas as pl
from jax.experimental.pallas import tpu as pltpu
from jax.sharding import PartitionSpec as P

REACH = 128
NORM_EPSILON = 0.1
MESH = pl.DeviceIdType.MESH


def bucket_table(length, bucket_count, reach_limit):
    offset = np.arange(length)[None, :] - np.arange(length)[:, None]
    half_count = bucket_count // 2
    upper_side = (offset > 0).astype(np.int32) * half_count
    distance = np.abs(offset)
    exact_count = half_count // 2
    scaled = (
        np.log(np.maximum(distance, 1) / exact_count)
        / np.log(reach_limit / exact_count)
        * (half_count - exact_count)
    )
    far_bucket = np.minimum(exact_count + scaled.astype(np.int32), half_count - 1)
    return (upper_side + np.where(distance < exact_count, distance, far_bucket)).astype(np.int32)


def relay_chunks(micro, micros, length):
    half = length // 2
    if micro == micros - 1:
        return [], (0, half), (half, length - half)
    return [(0, half), (half, length - half)], (0, 0), (0, 0)


def head_group(heads, head_size):
    return max(g for g in range(1, heads + 1) if heads % g == 0 and g * head_size <= 256)


def kernel(
    sizes,
    x_ref, gain_ref, bucket_ref, pbias_ref, wq_hbm, wo_hbm,
    o_ref,
    pre, xg, hg, spread, ho, fin, wq, wo, acc, sq, qkv, bias, head_mask,
    wq_sem, wo_sem,
    pre_recv, pre_send, pre_up, in_recv,
    hop_send, hop_recv, hop_line,
    spread_recv, spread_send, spread_up, late_recv, straight_send, straight_recv,
    mix_recv, mix_send,
    fin_send, fin_recv,
):
    S, M, L, H, hs = sizes
    Dl = x_ref.shape[1]
    Wl = H * hs
    G = head_group(H, hs)
    Wg = G * hs
    D = M * Dl
    s = lax.axis_index("section")
    m = lax.axis_index("mp")
    plans = [relay_chunks(i, S, L) for i in range(S)]

    def to(src, dst, send, recv, sec, col):
        return pltpu.make_async_remote_copy(
            src_ref=src, dst_ref=dst, send_sem=send, recv_sem=recv,
            device_id={"section": sec, "mp": col}, device_id_type=MESH,
        )

    def along(j, src, dst, send, recv, act):
        even = lax.rem(m - j + 2 * M, 2) == 0
        for reach in (2, 1):
            @pl.when((j <= m) & even & (m < M - reach))
            def _():
                act(to(src, dst, send.at[reach - 1, j], recv, s, m + reach))

            @pl.when((j >= m) & even & (m >= reach))
            def _():
                act(to(src, dst, send.at[reach + 1, j], recv, s, m - reach))

    def start(c):
        c.start()

    def sent(c):
        c.wait_send()

    def got(dst, recv):
        to(dst, dst, fin_send.at[0], recv, s, lax.rem(m + 1, M)).wait_recv()

    near = jnp.minimum(m, M - 1 - m)
    longer = jnp.where(m > M - 1 - m, -1, 1)

    def nth(p):
        k = (p + 1) // 2
        both = jnp.where(p % 2 == 1, -k, k)
        return m + jnp.where(p <= 2 * near, both, longer * (p - near))

    def wq_copy(j):
        rows = pl.ds(pl.multiple_of(j * Dl, Dl), Dl)
        return pltpu.make_async_copy(wq_hbm.at[:, rows, :], wq.at[:, rows, :], wq_sem.at[j])

    def wo_copy():
        return pltpu.make_async_copy(wo_hbm, wo, wo_sem)

    barrier = pltpu.get_barrier_semaphore()
    for o in range(S):
        for k in range(M):
            if o or k:
                pl.semaphore_signal(
                    barrier, inc=1,
                    device_id={"section": lax.rem(s + o, S), "mp": lax.rem(m + k, M)},
                    device_id_type=MESH,
                )

    for p in range(M):
        wq_copy(nth(p)).start()
    wo_copy().start()
    pl.semaphore_wait(barrier, S * M - 1)

    half = L // 2
    halves = [pl.ds(0, half), pl.ds(half, L - half)]

    def up_rows(j, c):
        return xg.at[j, pl.ds(pl.multiple_of(s * L + c * half, half), halves[c].size), :]

    def pre_part(j, c, src, act):
        along(j, src, pre.at[j, halves[c], :], pre_send.at[c], pre_recv.at[c, j], act)

        @pl.when(s > 0)
        def _():
            act(to(src, up_rows(j, c), pre_up.at[c, j], in_recv.at[s, c, j], 0, m))

    def first_act(act):
        for c in range(2):
            pre_part(m, c, x_ref.at[halves[c], :], act)

    def pre_act(j, act):
        for c in range(2):
            pre_part(j, c, pre.at[j, halves[c], :], act)

    def pre_step_on(j):
        for c in range(2):
            got(pre.at[j, halves[c], :], pre_recv.at[c, j])
            pre_part(j, c, pre.at[j, halves[c], :], start)

    first_act(start)

    for g in range(H // G):
        heads = []
        for h in range(g * G, (g + 1) * G):
            total = jnp.zeros(bucket_ref.shape, jnp.float32)
            for b in range(pbias_ref.shape[1]):
                total = jnp.where(bucket_ref[...] == b, pbias_ref[h, b], total)
            heads.append(total)
        bias[g] = jnp.concatenate(heads, axis=1)
    head_mask[...] = jnp.where(
        lax.broadcasted_iota(jnp.int32, (G * L, Wg), 0) // L
        == lax.broadcasted_iota(jnp.int32, (G * L, Wg), 1) // hs,
        1.0,
        0.0,
    ).astype(jnp.bfloat16)

    @pl.when(s > 0)
    def _():
        def pre_step(p, carry):
            j = nth(p)
            pre_step_on(j)
            return carry

        lax.fori_loop(1, M, pre_step, 0)

    def hop_block(i, c, j):
        at, rows = plans[i][0][c]
        return xg.at[j, pl.ds(i * L + at, rows), :]

    def hop_act(i, c, j, act):
        block = hop_block(i, c, j)
        along(j, block, block, hop_line.at[i, c], hop_recv.at[i, c, j], act)

    def late_block(i, j):
        at, rows = plans[i][1]
        return xg.at[j, pl.ds(i * L + at, rows), :]

    def straight_block(i, j):
        at, rows = plans[i][2]
        return xg.at[j, pl.ds(i * L + at, rows), :]

    def spread_block(i, j):
        return spread.at[i, j, pl.ds(0, plans[i][1][1]), :]

    def receive(i, j):
        @pl.when(s == 0)
        def _():
            if i:
                for c in range(2):
                    got(xg.at[j, pl.ds(i * L + c * half, halves[c].size), :], in_recv.at[i, c, j])
            else:
                @pl.when(j == m)
                def _():
                    xg[m, 0:L, :] = x_ref[...]

                @pl.when(j != m)
                def _():
                    pre_step_on(j)
                    xg[j, 0:L, :] = pre[j]

        @pl.when(s > 0)
        def _():
            for c in range(len(plans[i][0])):
                got(hop_block(i, c, j), hop_recv.at[i, c, j])
                hop_act(i, c, j, start)
            if plans[i][1][1]:
                got(late_block(i, j), late_recv.at[i, j])
            if plans[i][2][1]:
                got(straight_block(i, j), straight_recv.at[i, j])

    def mix_act(i, act):
        block = hg.at[pl.ds(i * L, L), pl.ds(pl.multiple_of(m * Wl, Wl), Wl)]
        for k in range(1, M):
            col = lax.rem(m + k, M)
            act(to(block, block, mix_send.at[i, k], mix_recv.at[i, m], s, col))

    scale = 1.0 / math.sqrt(hs)
    lane_head = lax.broadcasted_iota(jnp.int32, (L, Wg), 1) // hs

    def attend(i):
        for g in range(H // G):
            q = qkv[:, g * Wg : (g + 1) * Wg]
            k = qkv[:, Wl + g * Wg : Wl + (g + 1) * Wg]
            v = qkv[:, 2 * Wl + g * Wg : 2 * Wl + (g + 1) * Wg]
            apart = jnp.concatenate([q] * G, axis=0) * head_mask[...]
            scores = lax.dot_general(
                k, apart, (((1,), (1,)), ((), ())), preferred_element_type=jnp.float32
            ) * scale + bias[g]
            weights = jnp.exp(scores - jnp.max(scores, axis=0, keepdims=True))
            probs = (weights / jnp.sum(weights, axis=0, keepdims=True)).astype(jnp.bfloat16)
            mixed = lax.dot_general(
                probs, v, (((0,), (0,)), ((), ())), preferred_element_type=jnp.float32
            )
            out = mixed[0:L]
            for h in range(1, G):
                out = jnp.where(lane_head == h, mixed[h * L : (h + 1) * L], out)
            cols = pl.ds(pl.multiple_of(m * Wl + g * Wg, Wg), Wg)
            hg[i * L : (i + 1) * L, cols] = out.astype(jnp.bfloat16)

    for i in range(S):
        acc[...] = jnp.zeros_like(acc)
        sq[...] = jnp.zeros_like(sq)

        def qkv_step(p, carry):
            j = nth(p)
            receive(i, j)
            if i == 0:
                wq_copy(j).wait()
            block = xg[j, i * L : (i + 1) * L, :].astype(jnp.float32)
            squares = block * block
            part = squares[:, 0:128]
            for k in range(1, Dl // 128):
                part = part + squares[:, k * 128 : (k + 1) * 128]
            sq[...] += part
            rows = pl.ds(pl.multiple_of(j * Dl, Dl), Dl)
            gained = (block * gain_ref[:, rows].astype(jnp.float32)).astype(jnp.bfloat16)
            for t in range(3):
                cols = pl.ds(t * Wl, Wl)
                acc[:, cols] += jnp.dot(gained, wq[t, rows, :], preferred_element_type=jnp.float32)
            return carry

        lax.fori_loop(0, M, qkv_step, 0)
        row_scale = lax.rsqrt(jnp.sum(sq[...], axis=1, keepdims=True) / D + NORM_EPSILON)
        qkv[...] = (acc[...] * row_scale).astype(jnp.bfloat16)
        attend(i)
        mix_act(i, start)

    wo_copy().wait()

    def hop_out(i, act):
        for c, (at, rows) in enumerate(plans[i][0]):
            act(to(ho.at[pl.ds(i * L + at, rows), :], hop_block(i, c, m),
                   hop_send.at[i, c], hop_recv.at[i, c, m], s + 1, m))

    def late_out(i, j, src, act):
        along(j, src, spread_block(i, j), spread_send.at[i], spread_recv.at[i, j], act)
        act(to(src, late_block(i, j), spread_up.at[i, j], late_recv.at[i, j], s + 1, m))

    def straight_out(i, act):
        at, rows = plans[i][2]
        for k in range(M):
            act(to(ho.at[pl.ds(i * L + at, rows), :], straight_block(i, m),
                   straight_send.at[i, k], straight_recv.at[i, m], s + 1, lax.rem(m + k, M)))

    def own_late(i):
        at, rows = plans[i][1]
        return ho.at[pl.ds(i * L + at, rows), :]

    def home(i, act):
        act(to(ho.at[pl.ds(i * L, L), :], fin, fin_send.at[i], fin_recv, i, m))

    for i in range(S):
        for k in range(1, M):
            j = lax.rem(m + k, M)
            got(hg.at[pl.ds(i * L, L), pl.ds(pl.multiple_of(j * Wl, Wl), Wl)], mix_recv.at[i, j])
        rows = slice(i * L, (i + 1) * L)
        update = jnp.dot(hg[rows, :], wo[...], preferred_element_type=jnp.float32)
        ho[rows, :] = (xg[m, rows, :].astype(jnp.float32) + update).astype(jnp.bfloat16)

        @pl.when(s < S - 1)
        def _():
            hop_out(i, start)
            if plans[i][1][1]:
                late_out(i, m, own_late(i), start)
            if plans[i][2][1]:
                straight_out(i, start)
            if plans[i][1][1]:

                def late_step(p, carry):
                    j = nth(p)
                    got(spread_block(i, j), spread_recv.at[i, j])
                    late_out(i, j, spread_block(i, j), start)
                    return carry

                lax.fori_loop(1, M, late_step, 0)

        if i < S - 1:
            @pl.when(s == S - 1)
            def _():
                home(i, start)

    first_act(sent)
    for i in range(S):
        mix_act(i, sent)

        @pl.when(s > 0)
        def _():
            for c in range(len(plans[i][0])):
                hop_act(i, c, m, sent)

        @pl.when(s < S - 1)
        def _():
            hop_out(i, sent)
            if plans[i][1][1]:
                late_out(i, m, own_late(i), sent)
            if plans[i][2][1]:
                straight_out(i, sent)

        if i < S - 1:
            @pl.when(s == S - 1)
            def _():
                home(i, sent)

    def drain_step(p, carry):
        j = nth(p)
        pre_act(j, sent)
        for i in range(S):
            @pl.when(s > 0)
            def _():
                for c in range(len(plans[i][0])):
                    hop_act(i, c, j, sent)

            if plans[i][1][1]:
                @pl.when(s < S - 1)
                def _():
                    late_out(i, j, spread_block(i, j), sent)

        return carry

    lax.fori_loop(1, M, drain_step, 0)

    @pl.when(s == S - 1)
    def _():
        o_ref[...] = ho[(S - 1) * L :, :]

    @pl.when(s < S - 1)
    def _():
        got(fin, fin_recv)
        o_ref[...] = fin[...]


def solution(mesh):
    S, M = mesh.shape["section"], mesh.shape["mp"]

    def shards(micro_inputs, qkv_weight, out_weight, norm_gain, position_bias):
        L, Dl = micro_inputs.shape[1:]
        D = qkv_weight.shape[1]
        Wl = qkv_weight.shape[3]
        H = position_bias.shape[0]
        R = S * L
        G = head_group(H, Wl // H)
        plans = [relay_chunks(i, S, L) for i in range(S)]
        parts = max(1, *(len(hops) for hops, _, _ in plans))
        late_rows = max(rows for _, (_, rows), _ in plans)
        buckets = jnp.asarray(bucket_table(L, position_bias.shape[1], REACH).T)
        wq = jnp.transpose(qkv_weight[0], (1, 0, 2))
        bf16, f32 = jnp.bfloat16, jnp.float32
        dma = pltpu.SemaphoreType.DMA
        vmem = pl.BlockSpec(memory_space=pltpu.VMEM)
        out = pl.pallas_call(
            functools.partial(kernel, (S, M, L, H, Wl // H)),
            out_shape=jax.ShapeDtypeStruct((L, Dl), bf16),
            in_specs=[
                vmem, vmem, vmem, pl.BlockSpec(memory_space=pltpu.SMEM),
                pl.BlockSpec(memory_space=pltpu.HBM), pl.BlockSpec(memory_space=pltpu.HBM),
            ],
            out_specs=vmem,
            scratch_shapes=[
                pltpu.VMEM((M, L, Dl), bf16),
                pltpu.VMEM((M, R, Dl), bf16),
                pltpu.VMEM((R, M * Wl), bf16),
                pltpu.VMEM((S, M, late_rows, Dl), bf16),
                pltpu.VMEM((R, Dl), bf16),
                pltpu.VMEM((L, Dl), bf16),
                pltpu.VMEM((3, D, Wl), bf16),
                pltpu.VMEM((M * Wl, Dl), bf16),
                pltpu.VMEM((L, 3 * Wl), f32),
                pltpu.VMEM((L, 128), f32),
                pltpu.VMEM((L, 3 * Wl), bf16),
                pltpu.VMEM((H // G, L, G * L), f32),
                pltpu.VMEM((G * L, Wl // H * G), bf16),
                dma((M,)), dma,
                dma((2, M)), dma((2, 4, M)), dma((2, M)), dma((S, 2, M)),
                dma((S, parts)), dma((S, parts, M)), dma((S, parts, 4, M)),
                dma((S, M)), dma((S, 4, M)), dma((S, M)), dma((S, M)), dma((S, M)), dma((S, M)),
                dma((S, M)), dma((S, M)),
                dma((S,)), dma,
            ],
            compiler_params=pltpu.CompilerParams(
                collective_id=0, has_side_effects=True, vmem_limit_bytes=60 * 1024 * 1024
            ),
        )(micro_inputs[0], norm_gain, buckets, position_bias, wq, out_weight[0])
        return out[None]

    in_specs = (
        P(("dp", "section"), None, "mp"),
        P("section", None, None, "mp"),
        P("section", None, "mp"),
        P("section", None),
        P("mp", None),
    )
    out_specs = P(("dp", "section"), None, "mp")
    return jax.shard_map(shards, mesh=mesh, in_specs=in_specs, out_specs=out_specs, check_vma=False)
```

profile of v0, /device:TPU:0, one launch (start us, length us, event | category | flops | bytes accessed | tf_op | source)
XLA Modules:
  0.0 64.8 jit_solution(17519106335434247233)
XLA Ops:
  0.0 63.2 %shard_map.64 = bf16[64,1024]{1,0:T(8,128)(2,1)} custom-call(bf16[64,1024]{1,0:T(8,128)(2,1)} %bitcast.9, bf16[1,4096]{1,0:T(2,128)(2,1)} %gain_ref.1, s32[64,64]{1,0:T(8,128)} %constant.2.clone.bucket_ref, f32[8,32]{1,0:T(8,128)} %pbias_ref.1, bf16[3,4096,512]{2,1,0:T(8,128)(2,1)} %bitcast.6, bf16[2048,1024]{1,0:T(8,128)(2,1)} %bitcast.7), custom_call_target="tpu_custom_call" | custom-call | tf_op jit(solution)/shard_map/pallas_call | solution.py:397
  63.2 1.6 %copy.8 = bf16[1,64,1024]{2,1,0:T(8,128)(2,1)} copy(bf16[1,64,1024]{2,1,0:T(8,128)(2,1)} %bitcast.8) | data formatting | bytes 262144
where the time goes:
time: 64.9 us; the launch traced here: 64.8 us
  Pallas kernels  63.2 us (97%)
  local copies, waits for them, and re-layouts  1.57 us (2%)
    pallas_call x1, Pallas kernels, shards(): pl.pallas_call(functools.partial(kernel, (S, M, L, H, Wl // H)), out_shap...  63.2 us
    unnamed x1, local copies, waits for them, and re-layouts  1.57 us

commit v1 on v0

v1 whole, which is shorter than its diff:
```python
import functools
import math

import jax
import jax.numpy as jnp
import numpy as np
from jax import lax
from jax.experimental import pallas as pl
from jax.experimental.pallas import tpu as pltpu
from jax.sharding import PartitionSpec as P

REACH = 128
NORM_EPSILON = 0.1
MESH = pl.DeviceIdType.MESH
LAST_DETOUR = 3
EARLY = 1


def bucket_table(length, bucket_count, reach_limit):
    offset = np.arange(length)[None, :] - np.arange(length)[:, None]
    half_count = bucket_count // 2
    upper_side = (offset > 0).astype(np.int32) * half_count
    distance = np.abs(offset)
    exact_count = half_count // 2
    scaled = (
        np.log(np.maximum(distance, 1) / exact_count)
        / np.log(reach_limit / exact_count)
        * (half_count - exact_count)
    )
    far_bucket = np.minimum(exact_count + scaled.astype(np.int32), half_count - 1)
    return (upper_side + np.where(distance < exact_count, distance, far_bucket)).astype(np.int32)


def head_group(heads, head_size):
    return max(g for g in range(1, heads + 1) if heads % g == 0 and g * head_size <= 256)


def column_parts(width):
    return 2 if width % 256 == 0 else 1


def kernel(
    sizes,
    x_ref, gain_ref, bucket_ref, pbias_ref, wq_hbm, wo_hbm,
    o_ref,
    xg, hg, transit, ho, fin, wq, wo, acc, out_acc, sq, qkv, bias, head_mask,
    wq_sem, wo_sem,
    x_recv, line_send, first_send, up_send, straight_send, relay_send,
    mix_recv, mix_send, transit_recv, transit_up, transit_send,
    fin_send, fin_recv,
):
    S, M, L, H, hs = sizes
    C, _, Dc = ho.shape
    _, parts, _, Wp = transit.shape
    Dl = x_ref.shape[1]
    Wl = H * hs
    G = head_group(H, hs)
    Wg = G * hs
    D = M * Dl
    s = lax.axis_index("section")
    m = lax.axis_index("mp")

    def to(src, dst, send, recv, sec, col):
        return pltpu.make_async_remote_copy(
            src_ref=src, dst_ref=dst, send_sem=send, recv_sem=recv,
            device_id={"section": sec, "mp": col}, device_id_type=MESH,
        )

    def start(c):
        c.start()

    def sent(c):
        c.wait_send()

    def got(dst, recv):
        to(dst, dst, fin_send.at[0], recv, s, lax.rem(m + 1, M)).wait_recv()

    near = jnp.minimum(m, M - 1 - m)
    longer = jnp.where(m > M - 1 - m, -1, 1)

    def nth(p):
        k = (p + 1) // 2
        both = jnp.where(p % 2 == 1, -k, k)
        return m + jnp.where(p <= 2 * near, both, longer * (p - near))

    def others(body):
        def step(p, carry):
            j = nth(p)
            body(j, jnp.abs(j - m))
            return carry

        lax.fori_loop(1, M, step, 0)

    def others_far_first(body):
        def step(p, carry):
            j = nth(M - p)
            body(j, jnp.abs(j - m))
            return carry

        lax.fori_loop(1, M, step, 0)

    def wq_copy(j):
        rows = pl.ds(pl.multiple_of(j * Dl, Dl), Dl)
        return pltpu.make_async_copy(wq_hbm.at[:, rows, :], wq.at[:, rows, :], wq_sem.at[j])

    def wo_copy():
        return pltpu.make_async_copy(wo_hbm, wo, wo_sem)

    barrier = pltpu.get_barrier_semaphore()
    for o in range(S):
        for k in range(M):
            if o or k:
                pl.semaphore_signal(
                    barrier, inc=1,
                    device_id={"section": lax.rem(s + o, S), "mp": lax.rem(m + k, M)},
                    device_id_type=MESH,
                )

    for p in range(M):
        wq_copy(nth(p)).start()
    wo_copy().start()
    pl.semaphore_wait(barrier, S * M - 1)

    def rows_of(i):
        return pl.ds(i * L, L)

    def x_part(c):
        return x_ref.at[:, pl.ds(c * Dc, Dc)]

    def block(i, c, j):
        return xg.at[j, c, rows_of(i), :]

    def along(j, c, src, act):
        dst = block(0, c, j)
        even = lax.rem(m - j + 2 * M, 2) == 0
        for reach in (2, 1):
            @pl.when((j <= m) & even & (m < M - reach))
            def _():
                act(to(src, dst, line_send.at[c, reach - 1, j], x_recv.at[0, c, j], s, m + reach))

            @pl.when((j >= m) & even & (m >= reach))
            def _():
                act(to(src, dst, line_send.at[c, reach + 1, j], x_recv.at[0, c, j], s, m - reach))

    def first_out(act):
        def one(i, c, j):
            dst = xg.at[m, c, pl.ds(pl.multiple_of(i * L, L), L), :]
            act(to(x_part(c), dst, first_send.at[c, j], x_recv.at[i, c, m], 0, j))

        for c in range(C):
            one(s, c, m)
            others_far_first(lambda j, d: one(s, c, j))

    @pl.when(s == 0)
    def _():
        for c in range(C):
            along(m, c, x_part(c), start)

    @pl.when(s > 0)
    def _():
        first_out(start)

    for g in range(H // G):
        heads = []
        for h in range(g * G, (g + 1) * G):
            total = jnp.zeros(bucket_ref.shape, jnp.float32)
            for b in range(pbias_ref.shape[1]):
                total = jnp.where(bucket_ref[...] == b, pbias_ref[h, b], total)
            heads.append(total)
        bias[g] = jnp.concatenate(heads, axis=1)
    head_mask[...] = jnp.where(
        lax.broadcasted_iota(jnp.int32, (G * L, Wg), 0) // L
        == lax.broadcasted_iota(jnp.int32, (G * L, Wg), 1) // hs,
        1.0,
        0.0,
    ).astype(jnp.bfloat16)

    pair = s + 1 - 2 * lax.rem(s, 2)
    paired = pair < S

    def detour_from(i, row):
        return jnp.where((lax.rem(row, 2) == 1) & (i == S - 1), LAST_DETOUR, 3)

    def detoured(i, row, d):
        return paired & (d >= detour_from(i, row))

    def mix_part(i, g, j):
        return hg.at[rows_of(i), pl.ds(pl.multiple_of(j * Wl + g * Wp, Wp), Wp)]

    def far_reach(i, row):
        return paired & (jnp.maximum(m, M - 1 - m) >= detour_from(i, row))

    def mix_act(i, g, act):
        src = mix_part(i, g, m)

        @pl.when(far_reach(i, s))
        def _():
            act(to(src, transit.at[i, g], transit_up.at[i, g], transit_recv.at[i, g], pair, m))

        def one(j, d):
            @pl.when(jnp.logical_not(detoured(i, s, d)))
            def _():
                act(to(src, src, mix_send.at[i, g, j], mix_recv.at[i, g, m], s, j))

        others_far_first(one)

    def transit_act(i, g, act):
        def one(j, d):
            @pl.when(detoured(i, pair, d))
            def _():
                act(to(transit.at[i, g], mix_part(i, g, m), transit_send.at[i, g, j],
                       mix_recv.at[i, g, m], pair, j))

        others(one)

    def transit_all(act, wait):
        for i in range(S):
            @pl.when(far_reach(i, pair))
            def _():
                for g in range(parts):
                    if wait:
                        got(transit.at[i, g], transit_recv.at[i, g])
                    transit_act(i, g, act)

    def relay_act(i, c, act):
        def one(j, d):
            @pl.when(lax.rem(d, 2) == 1)
            def _():
                act(to(block(i, c, m), block(i, c, m), relay_send.at[i, c, j], x_recv.at[i, c, m], s, j))

        others_far_first(one)

    def relay(i):
        for c in range(C):
            got(block(i, c, m), x_recv.at[i, c, m])
            relay_act(i, c, start)

    @pl.when(lax.rem(s, 2) == 1)
    def _():
        transit_all(start, True)

    scale = 1.0 / math.sqrt(hs)
    lane_head = lax.broadcasted_iota(jnp.int32, (L, Wg), 1) // hs

    def attend(i):
        for g in range(H // G):
            q = qkv[:, g * Wg : (g + 1) * Wg]
            k = qkv[:, Wl + g * Wg : Wl + (g + 1) * Wg]
            v = qkv[:, 2 * Wl + g * Wg : 2 * Wl + (g + 1) * Wg]
            apart = jnp.concatenate([q] * G, axis=0) * head_mask[...]
            scores = lax.dot_general(
                k, apart, (((1,), (1,)), ((), ())), preferred_element_type=jnp.float32
            ) * scale + bias[g]
            weights = jnp.exp(scores - jnp.max(scores, axis=0, keepdims=True))
            probs = (weights / jnp.sum(weights, axis=0, keepdims=True)).astype(jnp.bfloat16)
            mixed = lax.dot_general(
                probs, v, (((0,), (0,)), ((), ())), preferred_element_type=jnp.float32
            )
            out = mixed[0:L]
            for h in range(1, G):
                out = jnp.where(lane_head == h, mixed[h * L : (h + 1) * L], out)
            cols = pl.ds(pl.multiple_of(m * Wl + g * Wg, Wg), Wg)
            hg[i * L : (i + 1) * L, cols] = out.astype(jnp.bfloat16)
            if parts > 1:
                mix_act(i, g, start)
        if parts == 1:
            mix_act(i, 0, start)

    def qkv_block(i, c, j):
        part_block = xg[j, c, i * L : (i + 1) * L, :].astype(jnp.float32)
        squares = part_block * part_block
        part = squares[:, 0:128]
        for k in range(1, Dc // 128):
            part = part + squares[:, k * 128 : (k + 1) * 128]
        sq[...] += part
        rows = pl.ds(pl.multiple_of(j * Dl + c * Dc, Dc), Dc)
        gained = (part_block * gain_ref[:, rows].astype(jnp.float32)).astype(jnp.bfloat16)
        for t in range(3):
            cols = pl.ds(t * Wl, Wl)
            acc[:, cols] += jnp.dot(gained, wq[t, rows, :], preferred_element_type=jnp.float32)

    for i in range(S):
        acc[...] = jnp.zeros_like(acc)
        sq[...] = jnp.zeros_like(sq)

        if i == 0:
            @pl.when(s == 0)
            def _():
                for c in range(C):
                    xg[m, c, 0:L, :] = x_ref[:, c * Dc : (c + 1) * Dc]

            @pl.when(s > 0)
            def _():
                relay(0)

        def qkv_step(p, carry):
            j = nth(p)
            if i == 0:
                wq_copy(j).wait()
            for c in range(C):
                @pl.when((j != m) | (s == 0) & (i > 0))
                def _():
                    got(block(i, c, j), x_recv.at[i, c, j])
                    if i == 0:
                        @pl.when(s == 0)
                        def _():
                            along(j, c, block(0, c, j), start)
                qkv_block(i, c, j)
            return carry

        early = min(EARLY, M)
        lax.fori_loop(0, early, qkv_step, 0)
        if i < S - 1:
            @pl.when(s > 0)
            def _():
                relay(i + 1)
        lax.fori_loop(early, M, qkv_step, 0)
        row_scale = lax.rsqrt(jnp.sum(sq[...], axis=1, keepdims=True) / D + NORM_EPSILON)
        qkv[...] = (acc[...] * row_scale).astype(jnp.bfloat16)
        attend(i)

    wo_copy().wait()

    def ho_part(i, c):
        return ho.at[c, rows_of(i), :]

    def up_act(i, c, act):
        act(to(ho_part(i, c), block(i, c, m), up_send.at[i, c], x_recv.at[i, c, m], s + 1, m))

    def straight_act(i, c, act):
        def one(j, d):
            @pl.when(lax.rem(d, 2) == 0)
            def _():
                act(to(ho_part(i, c), block(i, c, m), straight_send.at[i, c, j], x_recv.at[i, c, m], s + 1, j))

        others_far_first(one)

    def home(i, act):
        act(to(ho.at[:, rows_of(i), :], fin, fin_send.at[i], fin_recv, i, m))

    for i in range(S):
        def out_step(p, carry):
            j = nth(p)

            @pl.when(j != m)
            def _():
                for g in range(parts):
                    got(mix_part(i, g, j), mix_recv.at[i, g, j])
            cols = pl.ds(pl.multiple_of(j * Wl, Wl), Wl)
            update = jnp.dot(hg[i * L : (i + 1) * L, cols], wo[cols, :], preferred_element_type=jnp.float32)
            out_acc[...] = jnp.where(p == 0, update, out_acc[...] + update)
            return carry

        lax.fori_loop(0, M, out_step, 0)
        for c in range(C):
            total = xg[m, c, i * L : (i + 1) * L, :].astype(jnp.float32) + out_acc[:, c * Dc : (c + 1) * Dc]
            ho[c, i * L : (i + 1) * L, :] = total.astype(jnp.bfloat16)

            @pl.when(s < S - 1)
            def _():
                up_act(i, c, start)

        @pl.when(s < S - 1)
        def _():
            for c in range(C):
                straight_act(i, c, start)

        if i < S - 1:
            @pl.when(s == S - 1)
            def _():
                home(i, start)

    @pl.when(lax.rem(s, 2) == 0)
    def _():
        transit_all(start, True)

    @pl.when(s == 0)
    def _():
        for c in range(C):
            along(m, c, x_part(c), sent)
            others(lambda j, d: along(j, c, block(0, c, j), sent))

    @pl.when(s > 0)
    def _():
        first_out(sent)

    for i in range(S):
        for g in range(parts):
            mix_act(i, g, sent)

        @pl.when(s > 0)
        def _():
            for c in range(C):
                relay_act(i, c, sent)

        @pl.when(s < S - 1)
        def _():
            for c in range(C):
                up_act(i, c, sent)
                straight_act(i, c, sent)

        if i < S - 1:
            @pl.when(s == S - 1)
            def _():
                home(i, sent)

    transit_all(sent, False)

    @pl.when(s == S - 1)
    def _():
        for c in range(C):
            o_ref[:, c * Dc : (c + 1) * Dc] = ho[c, (S - 1) * L :, :]

    @pl.when(s < S - 1)
    def _():
        got(fin, fin_recv)
        for c in range(C):
            o_ref[:, c * Dc : (c + 1) * Dc] = fin[c]


def solution(mesh):
    S, M = mesh.shape["section"], mesh.shape["mp"]

    def shards(micro_inputs, qkv_weight, out_weight, norm_gain, position_bias):
        L, Dl = micro_inputs.shape[1:]
        D = qkv_weight.shape[1]
        Wl = qkv_weight.shape[3]
        H = position_bias.shape[0]
        R = S * L
        hs = Wl // H
        G = head_group(H, hs)
        N = H // G
        parts = N
        C = column_parts(Dl)
        buckets = jnp.asarray(bucket_table(L, position_bias.shape[1], REACH).T)
        wq = jnp.transpose(qkv_weight[0], (1, 0, 2))
        bf16, f32 = jnp.bfloat16, jnp.float32
        dma = pltpu.SemaphoreType.DMA
        vmem = pl.BlockSpec(memory_space=pltpu.VMEM)
        out = pl.pallas_call(
            functools.partial(kernel, (S, M, L, H, hs)),
            out_shape=pltpu.VMEM((L, Dl), bf16),
            in_specs=[
                vmem, vmem, vmem, pl.BlockSpec(memory_space=pltpu.SMEM),
                pl.BlockSpec(memory_space=pltpu.HBM), pl.BlockSpec(memory_space=pltpu.HBM),
            ],
            out_specs=vmem,
            scratch_shapes=[
                pltpu.VMEM((M, C, R, Dl // C), bf16),
                pltpu.VMEM((R, M * Wl), bf16),
                pltpu.VMEM((S, parts, L, Wl // parts), bf16),
                pltpu.VMEM((C, R, Dl // C), bf16),
                pltpu.VMEM((C, L, Dl // C), bf16),
                pltpu.VMEM((3, D, Wl), bf16),
                pltpu.VMEM((M * Wl, Dl), bf16),
                pltpu.VMEM((L, 3 * Wl), f32),
                pltpu.VMEM((L, Dl), f32),
                pltpu.VMEM((L, 128), f32),
                pltpu.VMEM((L, 3 * Wl), bf16),
                pltpu.VMEM((N, L, G * L), f32),
                pltpu.VMEM((G * L, G * hs), bf16),
                dma((M,)), dma,
                dma((S, C, M)), dma((C, 4, M)), dma((C, M)), dma((S, C)), dma((S, C, M)), dma((S, C, M)),
                dma((S, parts, M)), dma((S, parts, M)), dma((S, parts)), dma((S, parts)), dma((S, parts, M)),
                dma((S,)), dma,
            ],
            compiler_params=pltpu.CompilerParams(
                collective_id=0, has_side_effects=True, vmem_limit_bytes=60 * 1024 * 1024
            ),
        )(micro_inputs[0], norm_gain, buckets, position_bias, wq, out_weight[0])
        return out[None]

    in_specs = (
        P(("dp", "section"), None, "mp"),
        P("section", None, None, "mp"),
        P("section", None, "mp"),
        P("section", None),
        P("mp", None),
    )
    out_specs = P(("dp", "section"), None, "mp")
    return jax.shard_map(shards, mesh=mesh, in_specs=in_specs, out_specs=out_specs, check_vma=False)
```

time: 64.9 us -> 59.9 us (0.923)
  Pallas kernels: 63.2 us -> 59 us
  local copies, waits for them, and re-layouts: 1.57 us -> 0.66 us
    pallas_call x1, Pallas kernels: 63.2 us -> 59 us  [shards(): pl.pallas_call(functools.partial(kernel, (S, M, L, H, hs)), out_shape=plt...]
    unnamed x1, local copies, waits for them, and re-layouts: 1.57 us -> 0.66 us
where the time goes in v1:
time: 59.9 us; the launch traced here: 59.7 us
  Pallas kernels  59 us (98%)
  local copies, waits for them, and re-layouts  0.66 us (1%)
    pallas_call x1, Pallas kernels, shards(): pl.pallas_call(functools.partial(kernel, (S, M, L, H, hs)), out_shape=plt...  59 us

profile of v1, /device:TPU:0, one launch (start us, length us, event | category | flops | bytes accessed | tf_op | source)
XLA Modules:
  0.0 59.7 jit_solution(13049426630137507390)
XLA Ops:
  0.0 59.0 %shard_map.64 = bf16[64,1024]{1,0:T(8,128)(2,1)S(1)} custom-call(bf16[64,1024]{1,0:T(8,128)(2,1)} %bitcast.9, bf16[1,4096]{1,0:T(2,128)(2,1)} %gain_ref.1, s32[64,64]{1,0:T(8,128)} %constant.2.clone.bucket_ref, f32[8,32]{1,0:T(8,128)} %pbias_ref.1, bf16[3,4096,512]{2,1,0:T(8,128)(2,1)} %bitcast.7, bf16[2048,1024]{1,0:T(8,128)(2,1)} %bitcast.8), custom_call_target="tpu_custom_call" | custom-call | tf_op jit(solution)/shard_map/pallas_call | solution.py:440
  59.0 0.7 %copy.8 = bf16[1,64,1024]{2,1,0:T(8,128)(2,1)} copy(bf16[1,64,1024]{2,1,0:T(8,128)(2,1)S(1)} %bitcast.6) | data formatting | bytes 262144

commit v2 on v1

--- a/solution.py
+++ b/solution.py
@@ -82,6 +82,11 @@
         k = (p + 1) // 2
         both = jnp.where(p % 2 == 1, -k, k)
         return m + jnp.where(p <= 2 * near, both, longer * (p - near))
+
+    hand_on = jnp.where(near > 0, 3, 2) if M > 3 else 1
+
+    def relay_first(p):
+        return nth(jnp.where(p == 1, hand_on, jnp.where((p > 1) & (p <= hand_on), p - 1, p)))
 
     def others(body):
         def step(p, carry):
@@ -294,7 +299,7 @@
                 relay(0)
 
         def qkv_step(p, carry):
-            j = nth(p)
+            j = jnp.where(s == 0, relay_first(p), nth(p)) if i == 0 else nth(p)
             if i == 0:
                 wq_copy(j).wait()
             for c in range(C):

time: 59.9 us -> 54 us (0.902)
  Pallas kernels: 59 us -> 53.2 us
    pallas_call x1, Pallas kernels: 59 us -> 53.2 us  [shards(): pl.pallas_call(functools.partial(kernel, (S, M, L, H, hs)), out_shape=plt...]
where the time goes in v2:
time: 54 us; the launch traced here: 53.9 us
  Pallas kernels  53.2 us (99%)
  local copies, waits for them, and re-layouts  0.66 us (1%)
    pallas_call x1, Pallas kernels, shards(): pl.pallas_call(functools.partial(kernel, (S, M, L, H, hs)), out_shape=plt...  53.2 us

profile of v2, /device:TPU:0, one launch (start us, length us, event | category | flops | bytes accessed | tf_op | source)
XLA Modules:
  0.0 53.9 jit_solution(13882338922989683324)
XLA Ops:
  0.0 53.2 %shard_map.64 = bf16[64,1024]{1,0:T(8,128)(2,1)S(1)} custom-call(bf16[64,1024]{1,0:T(8,128)(2,1)} %bitcast.9, bf16[1,4096]{1,0:T(2,128)(2,1)} %gain_ref.1, s32[64,64]{1,0:T(8,128)} %constant.2.clone.bucket_ref, f32[8,32]{1,0:T(8,128)} %pbias_ref.1, bf16[3,4096,512]{2,1,0:T(8,128)(2,1)} %bitcast.7, bf16[2048,1024]{1,0:T(8,128)(2,1)} %bitcast.8), custom_call_target="tpu_custom_call" | custom-call | tf_op jit(solution)/shard_map/pallas_call | solution.py:445
  53.2 0.7 %copy.8 = bf16[1,64,1024]{2,1,0:T(8,128)(2,1)} copy(bf16[1,64,1024]{2,1,0:T(8,128)(2,1)S(1)} %bitcast.6) | data formatting | bytes 262144

commit v3 on v2

--- a/solution.py
+++ b/solution.py
@@ -14,6 +14,7 @@
 MESH = pl.DeviceIdType.MESH
 LAST_DETOUR = 3
 EARLY = 1
+NEAR = True
 
 
 def bucket_table(length, bucket_count, reach_limit):
@@ -43,9 +44,9 @@
     sizes,
     x_ref, gain_ref, bucket_ref, pbias_ref, wq_hbm, wo_hbm,
     o_ref,
-    xg, hg, transit, ho, fin, wq, wo, acc, out_acc, sq, qkv, bias, head_mask,
+    pre, xg, hg, transit, ho, fin, wq, wo, acc, out_acc, sq, qkv, bias, head_mask,
     wq_sem, wo_sem,
-    x_recv, line_send, first_send, up_send, straight_send, relay_send,
+    pre_recv, x_recv, line_send, down_send, up_send, straight_send, relay_send,
     mix_recv, mix_send, transit_recv, transit_up, transit_send,
     fin_send, fin_recv,
 ):
@@ -112,19 +113,36 @@
         return pltpu.make_async_copy(wo_hbm, wo, wo_sem)
 
     barrier = pltpu.get_barrier_semaphore()
-    for o in range(S):
-        for k in range(M):
-            if o or k:
-                pl.semaphore_signal(
-                    barrier, inc=1,
-                    device_id={"section": lax.rem(s + o, S), "mp": lax.rem(m + k, M)},
-                    device_id_type=MESH,
-                )
+
+    def greet(sec, col):
+        pl.semaphore_signal(barrier, inc=1, device_id={"section": sec, "mp": col}, device_id_type=MESH)
+
+    if NEAR and S <= 2:
+        if S == 2:
+            greet(1 - s, m)
+
+        greeted = S - 1
+        for reach in (1, 2):
+            @pl.when(m >= reach)
+            def _():
+                greet(s, m - reach)
+
+            @pl.when(m < M - reach)
+            def _():
+                greet(s, m + reach)
+
+            greeted = greeted + jnp.where(m >= reach, 1, 0) + jnp.where(m < M - reach, 1, 0)
+    else:
+        for o in range(S):
+            for k in range(M):
+                if o or k:
+                    greet(lax.rem(s + o, S), lax.rem(m + k, M))
+        greeted = S * M - 1
 
     for p in range(M):
         wq_copy(nth(p)).start()
     wo_copy().start()
-    pl.semaphore_wait(barrier, S * M - 1)
+    pl.semaphore_wait(barrier, greeted)
 
     def rows_of(i):
         return pl.ds(i * L, L)
@@ -135,35 +153,43 @@
     def block(i, c, j):
         return xg.at[j, c, rows_of(i), :]
 
-    def along(j, c, src, act):
-        dst = block(0, c, j)
+    def ring(c, j, src, dst, recv, act):
         even = lax.rem(m - j + 2 * M, 2) == 0
         for reach in (2, 1):
             @pl.when((j <= m) & even & (m < M - reach))
             def _():
-                act(to(src, dst, line_send.at[c, reach - 1, j], x_recv.at[0, c, j], s, m + reach))
+                act(to(src, dst, line_send.at[c, reach - 1, j], recv, s, m + reach))
 
             @pl.when((j >= m) & even & (m >= reach))
             def _():
-                act(to(src, dst, line_send.at[c, reach + 1, j], x_recv.at[0, c, j], s, m - reach))
-
-    def first_out(act):
-        def one(i, c, j):
-            dst = xg.at[m, c, pl.ds(pl.multiple_of(i * L, L), L), :]
-            act(to(x_part(c), dst, first_send.at[c, j], x_recv.at[i, c, m], 0, j))
-
-        for c in range(C):
-            one(s, c, m)
-            others_far_first(lambda j, d: one(s, c, j))
+                act(to(src, dst, line_send.at[c, reach + 1, j], recv, s, m - reach))
+
+    def along(c, j, src, act):
+        ring(c, j, src, block(0, c, j), x_recv.at[0, c, j], act)
+
+    def hop(c, j, src, dst, recv, act):
+        @pl.when((j <= m) & (m < M - 1))
+        def _():
+            act(to(src, dst, line_send.at[c, 0, j], recv, s, m + 1))
+
+        @pl.when((j >= m) & (m > 0))
+        def _():
+            act(to(src, dst, line_send.at[c, 1, j], recv, s, m - 1))
+
+    def down(c, j, src, act):
+        dst = xg.at[j, c, pl.ds(pl.multiple_of(s * L, L), L), :]
+        act(to(src, dst, down_send.at[c, j], x_recv.at[s, c, j], 0, m))
+        hop(c, j, src, pre.at[j, c], pre_recv.at[c, j], act)
 
     @pl.when(s == 0)
     def _():
         for c in range(C):
-            along(m, c, x_part(c), start)
+            along(c, m, x_part(c), start)
 
     @pl.when(s > 0)
     def _():
-        first_out(start)
+        for c in range(C):
+            down(c, m, x_part(c), start)
 
     for g in range(H // G):
         heads = []
@@ -179,6 +205,25 @@
         1.0,
         0.0,
     ).astype(jnp.bfloat16)
+
+    @pl.when(s > 0)
+    def _():
+        def hand_down(c, j):
+            got(pre.at[j, c], pre_recv.at[c, j])
+            down(c, j, pre.at[j, c], start)
+
+        def hand_step(d, carry):
+            for c in range(C):
+                @pl.when(m >= d)
+                def _():
+                    hand_down(c, m - d)
+
+                @pl.when(m < M - d)
+                def _():
+                    hand_down(c, m + d)
+            return carry
+
+        lax.fori_loop(1, M, hand_step, 0)
 
     pair = s + 1 - 2 * lax.rem(s, 2)
     paired = pair < S
@@ -299,7 +344,7 @@
                 relay(0)
 
         def qkv_step(p, carry):
-            j = jnp.where(s == 0, relay_first(p), nth(p)) if i == 0 else nth(p)
+            j = relay_first(p) if i == 0 else nth(p)
             if i == 0:
                 wq_copy(j).wait()
             for c in range(C):
@@ -309,7 +354,7 @@
                     if i == 0:
                         @pl.when(s == 0)
                         def _():
-                            along(j, c, block(0, c, j), start)
+                            along(c, j, block(0, c, j), start)
                 qkv_block(i, c, j)
             return carry
 
@@ -382,12 +427,14 @@
     @pl.when(s == 0)
     def _():
         for c in range(C):
-            along(m, c, x_part(c), sent)
-            others(lambda j, d: along(j, c, block(0, c, j), sent))
+            along(c, m, x_part(c), sent)
+            others(lambda j, d: along(c, j, block(0, c, j), sent))
 
     @pl.when(s > 0)
     def _():
-        first_out(sent)
+        for c in range(C):
+            down(c, m, x_part(c), sent)
+            others(lambda j, d: down(c, j, pre.at[j, c], sent))
 
     for i in range(S):
         for g in range(parts):
@@ -451,6 +498,7 @@
             ],
             out_specs=vmem,
             scratch_shapes=[
+                pltpu.VMEM((M, C, L, Dl // C), bf16),
                 pltpu.VMEM((M, C, R, Dl // C), bf16),
                 pltpu.VMEM((R, M * Wl), bf16),
                 pltpu.VMEM((S, parts, L, Wl // parts), bf16),
@@ -465,7 +513,7 @@
                 pltpu.VMEM((N, L, G * L), f32),
                 pltpu.VMEM((G * L, G * hs), bf16),
                 dma((M,)), dma,
-                dma((S, C, M)), dma((C, 4, M)), dma((C, M)), dma((S, C)), dma((S, C, M)), dma((S, C, M)),
+                dma((C, M)), dma((S, C, M)), dma((C, 4, M)), dma((C, M)), dma((S, C)), dma((S, C, M)), dma((S, C, M)),
                 dma((S, parts, M)), dma((S, parts, M)), dma((S, parts)), dma((S, parts)), dma((S, parts, M)),
                 dma((S,)), dma,
             ],

time: 54 us -> 53.4 us (0.989)
  Pallas kernels: 53.2 us -> 52.6 us
    pallas_call x1, Pallas kernels: 53.2 us -> 52.6 us  [shards(): pl.pallas_call(functools.partial(kernel, (S, M, L, H, hs)), out_shape=plt...]
where the time goes in v3:
time: 53.4 us; the launch traced here: 53.2 us
  Pallas kernels  52.6 us (99%)
  local copies, waits for them, and re-layouts  0.66 us (1%)
    pallas_call x1, Pallas kernels, shards(): pl.pallas_call(functools.partial(kernel, (S, M, L, H, hs)), out_shape=plt...  52.6 us

profile of v3, /device:TPU:0, one launch (start us, length us, event | category | flops | bytes accessed | tf_op | source)
XLA Modules:
  0.0 53.2 jit_solution(9765635582039279061)
XLA Ops:
  0.0 52.6 %shard_map.64 = bf16[64,1024]{1,0:T(8,128)(2,1)S(1)} custom-call(bf16[64,1024]{1,0:T(8,128)(2,1)} %bitcast.9, bf16[1,4096]{1,0:T(2,128)(2,1)} %gain_ref.1, s32[64,64]{1,0:T(8,128)} %constant.2.clone.bucket_ref, f32[8,32]{1,0:T(8,128)} %pbias_ref.1, bf16[3,4096,512]{2,1,0:T(8,128)(2,1)} %bitcast.7, bf16[2048,1024]{1,0:T(8,128)(2,1)} %bitcast.8), custom_call_target="tpu_custom_call" | custom-call | tf_op jit(solution)/shard_map/pallas_call | solution.py:492
  52.6 0.7 %copy.8 = bf16[1,64,1024]{2,1,0:T(8,128)(2,1)} copy(bf16[1,64,1024]{2,1,0:T(8,128)(2,1)S(1)} %bitcast.6) | data formatting | bytes 262144

commit v4 on v3

--- a/solution.py
+++ b/solution.py
@@ -74,7 +74,7 @@
         c.wait_send()
 
     def got(dst, recv):
-        to(dst, dst, fin_send.at[0], recv, s, lax.rem(m + 1, M)).wait_recv()
+        to(dst, dst, fin_send.at[0, 0], recv, s, lax.rem(m + 1, M)).wait_recv()
 
     near = jnp.minimum(m, M - 1 - m)
     longer = jnp.where(m > M - 1 - m, -1, 1)
@@ -385,8 +385,8 @@
 
         others_far_first(one)
 
-    def home(i, act):
-        act(to(ho.at[:, rows_of(i), :], fin, fin_send.at[i], fin_recv, i, m))
+    def home(i, c, act):
+        act(to(ho.at[c, rows_of(i), :], fin.at[c], fin_send.at[i, c], fin_recv.at[c], i, m))
 
     for i in range(S):
         def out_step(p, carry):
@@ -410,15 +410,15 @@
             def _():
                 up_act(i, c, start)
 
+            if i < S - 1:
+                @pl.when(s == S - 1)
+                def _():
+                    home(i, c, start)
+
         @pl.when(s < S - 1)
         def _():
             for c in range(C):
                 straight_act(i, c, start)
-
-        if i < S - 1:
-            @pl.when(s == S - 1)
-            def _():
-                home(i, start)
 
     @pl.when(lax.rem(s, 2) == 0)
     def _():
@@ -454,7 +454,8 @@
         if i < S - 1:
             @pl.when(s == S - 1)
             def _():
-                home(i, sent)
+                for c in range(C):
+                    home(i, c, sent)
 
     transit_all(sent, False)
 
@@ -465,8 +466,8 @@
 
     @pl.when(s < S - 1)
     def _():
-        got(fin, fin_recv)
-        for c in range(C):
+        for c in range(C):
+            got(fin.at[c], fin_recv.at[c])
             o_ref[:, c * Dc : (c + 1) * Dc] = fin[c]
 
 
@@ -515,7 +516,7 @@
                 dma((M,)), dma,
                 dma((C, M)), dma((S, C, M)), dma((C, 4, M)), dma((C, M)), dma((S, C)), dma((S, C, M)), dma((S, C, M)),
                 dma((S, parts, M)), dma((S, parts, M)), dma((S, parts)), dma((S, parts)), dma((S, parts, M)),
-                dma((S,)), dma,
+                dma((S, C)), dma((C,)),
             ],
             compiler_params=pltpu.CompilerParams(
                 collective_id=0, has_side_effects=True, vmem_limit_bytes=60 * 1024 * 1024

time: 53.4 us -> 53.4 us (level)
  no operation moved by 1% of the time
where the time goes in v4:
time: 53.4 us; the launch traced here: 53.2 us
  Pallas kernels  52.6 us (99%)
  local copies, waits for them, and re-layouts  0.66 us (1%)
    pallas_call x1, Pallas kernels, shards(): pl.pallas_call(functools.partial(kernel, (S, M, L, H, hs)), out_shape=plt...  52.6 us

profile of v4, /device:TPU:0, one launch (start us, length us, event | category | flops | bytes accessed | tf_op | source)
XLA Modules:
  0.0 53.2 jit_solution(12157720432208334891)
XLA Ops:
  0.0 52.6 %shard_map.64 = bf16[64,1024]{1,0:T(8,128)(2,1)S(1)} custom-call(bf16[64,1024]{1,0:T(8,128)(2,1)} %bitcast.9, bf16[1,4096]{1,0:T(2,128)(2,1)} %gain_ref.1, s32[64,64]{1,0:T(8,128)} %constant.2.clone.bucket_ref, f32[8,32]{1,0:T(8,128)} %pbias_ref.1, bf16[3,4096,512]{2,1,0:T(8,128)(2,1)} %bitcast.7, bf16[2048,1024]{1,0:T(8,128)(2,1)} %bitcast.8), custom_call_target="tpu_custom_call" | custom-call | tf_op jit(solution)/shard_map/pallas_call | solution.py:493
  52.6 0.7 %copy.8 = bf16[1,64,1024]{2,1,0:T(8,128)(2,1)} copy(bf16[1,64,1024]{2,1,0:T(8,128)(2,1)S(1)} %bitcast.6) | data formatting | bytes 262144
